TPU v7x, 32 devices: a whole 2x2x4 slice. The times are simulated.
32 devices in a mesh: batch: 4 (over x, core), seq: 8 (over z, y).
Axes of the slice: x: 2, y: 2, z: 4, core: 2. Of those that a mesh axis runs over, the one named last changes fastest.
Arguments:
- signal: bfloat16 [4, 2048, 256], P('batch', 'seq'), may hold values from -0.3125 to 0.3125
- grad_out: bfloat16 [4, 2048, 256], P('batch', 'seq'), may hold values from -6 to 6
- filter_taps: float32 [2048, 256], P('seq'), may hold values from -0.3125 to 0.3125
- skip_gain: float32 [256], replicated, may hold values from 0.5 to 2
Outputs:
- input_grad: bfloat16 [4, 2048, 256], P('batch', 'seq')
- filter_grad: float32 [2048, 256], P('seq')
All inputs are finite; a program needn't handle non-finite values.
Results may differ from a plain program's by a relative error of at most 0.001.
Values sent between devices are 32-bit elements; how exact they have to be, the bound alone decides.
A program may use at most 64 MiB of HBM per device.

v0:
```python
import jax
import jax.numpy as jnp
from jax import lax
from jax.sharding import PartitionSpec as P


def angle_table(height, width, period):
    product = lax.broadcasted_iota(jnp.int32, (height, width), 0) * lax.broadcasted_iota(
        jnp.int32, (height, width), 1
    )
    return 2.0 * jnp.pi / period * (product % period).astype(jnp.float32)


def angle_of(product, period):
    return 2.0 * jnp.pi / period * (product % period).astype(jnp.float32)


def coarse_order(slot, seq_count):
    pair_index = slot // 2
    odd_slot = slot % 2
    return jnp.where(
        pair_index == 0,
        odd_slot * seq_count,
        jnp.where(odd_slot == 0, pair_index, 2 * seq_count - pair_index),
    )


def contract(form, table, operand):
    return jnp.einsum(form, table, operand, precision=lax.Precision.HIGHEST)


def forward_spectra(columns):
    seq_count = lax.axis_size("seq")
    row_count = columns.shape[0]
    part_rows = row_count // seq_count
    period_len = 2 * row_count * seq_count
    spread = lax.all_to_all(
        columns.reshape(1, row_count, columns.shape[1]),
        "seq",
        split_axis=1,
        concat_axis=0,
        tiled=True,
    )
    slot_grid = lax.broadcasted_iota(jnp.int32, (2 * seq_count, seq_count), 0)
    source_grid = lax.broadcasted_iota(jnp.int32, (2 * seq_count, seq_count), 1)
    first_table = angle_of(coarse_order(slot_grid, seq_count) * source_grid, 2 * seq_count)
    cos_first = jnp.cos(first_table)
    sin_first = jnp.sin(first_table)
    half_width = spread.shape[2] // 2
    real_in = spread[:, :, :half_width]
    imag_in = spread[:, :, half_width:]
    real_part = contract("ks,srw->krw", cos_first, real_in) + contract(
        "ks,srw->krw", sin_first, imag_in
    )
    imag_part = contract("ks,srw->krw", cos_first, imag_in) - contract(
        "ks,srw->krw", sin_first, real_in
    )
    global_row = lax.axis_index("seq") * part_rows + lax.broadcasted_iota(
        jnp.int32, (2 * seq_count, part_rows), 1
    )
    coarse = coarse_order(lax.broadcasted_iota(jnp.int32, (2 * seq_count, part_rows), 0), seq_count)
    phases = angle_of(global_row * coarse, period_len)
    cos_turn = jnp.cos(phases)[:, :, None]
    sin_turn = jnp.sin(phases)[:, :, None]
    rotated = jnp.stack(
        [real_part * cos_turn + imag_part * sin_turn, imag_part * cos_turn - real_part * sin_turn]
    )
    inner_table = angle_table(row_count, row_count, row_count)
    cos_inner = jnp.cos(inner_table)
    sin_inner = jnp.sin(inner_table)
    pieces = lax.all_to_all(rotated, "seq", split_axis=1, concat_axis=2, tiled=True)
    real_sum = contract("qr,krw->kqw", cos_inner, pieces[0]) + contract(
        "qr,krw->kqw", sin_inner, pieces[1]
    )
    imag_sum = contract("qr,krw->kqw", cos_inner, pieces[1]) - contract(
        "qr,krw->kqw", sin_inner, pieces[0]
    )
    return jnp.stack([real_sum, imag_sum])


def split_pairs(packed):
    reversed_q = packed[:, :, ::-1]
    zero_row = jnp.roll(reversed_q[:, 0], 1, axis=1)
    own_pair = jnp.stack([zero_row, reversed_q[:, 1]], axis=1)
    partner = jnp.where(lax.axis_index("seq") == 0, own_pair, reversed_q[:, ::-1])
    first = jnp.stack([0.5 * (packed[0] + partner[0]), 0.5 * (packed[1] - partner[1])])
    second = jnp.stack([0.5 * (packed[1] + partner[1]), 0.5 * (partner[0] - packed[0])])
    return (first, second)


def inverse_rows(spectra):
    seq_count = lax.axis_size("seq")
    row_count = spectra.shape[2]
    period_len = 2 * row_count * seq_count
    inner_table = angle_table(row_count, row_count, row_count)
    cos_inner = jnp.cos(inner_table)
    sin_inner = jnp.sin(inner_table)
    real_sum = contract("qr,krw->kqw", cos_inner, spectra[0]) - contract(
        "qr,krw->kqw", sin_inner, spectra[1]
    )
    imag_sum = contract("qr,krw->kqw", cos_inner, spectra[1]) + contract(
        "qr,krw->kqw", sin_inner, spectra[0]
    )
    coarse = coarse_order(
        2 * lax.axis_index("seq") + lax.broadcasted_iota(jnp.int32, (2, row_count), 0), seq_count
    )
    position = lax.broadcasted_iota(jnp.int32, (2, row_count), 1)
    phases = angle_of(position * coarse, period_len)
    cos_turn = jnp.cos(phases)[:, :, None]
    sin_turn = jnp.sin(phases)[:, :, None]
    rotated = jnp.stack(
        [real_sum * cos_turn - imag_sum * sin_turn, real_sum * sin_turn + imag_sum * cos_turn]
    )
    target_grid = lax.broadcasted_iota(jnp.int32, (seq_count, 2 * seq_count), 0)
    slot_grid = lax.broadcasted_iota(jnp.int32, (seq_count, 2 * seq_count), 1)
    last_table = angle_of(target_grid * coarse_order(slot_grid, seq_count), 2 * seq_count)
    cos_last = jnp.cos(last_table)
    sin_last = jnp.sin(last_table)
    pieces = lax.all_to_all(rotated, "seq", split_axis=2, concat_axis=1, tiled=True)
    value = contract("sk,krw->srw", cos_last, pieces[0]) - contract(
        "sk,krw->srw", sin_last, pieces[1]
    )
    other = contract("sk,krw->srw", sin_last, pieces[0]) + contract(
        "sk,krw->srw", cos_last, pieces[1]
    )
    gathered = (value / period_len, other / period_len)
    gathered = jnp.concatenate([gathered[0], gathered[1]], axis=2)
    home_rows = lax.all_to_all(gathered, "seq", split_axis=0, concat_axis=1, tiled=True)
    return home_rows.reshape(row_count, home_rows.shape[2])


def invert_all(spectra):
    half_width = spectra.shape[3] // 2
    joined = jnp.stack(
        [
            spectra[0, :, :, :half_width] - spectra[1, :, :, half_width:],
            spectra[1, :, :, :half_width] + spectra[0, :, :, half_width:],
        ]
    )
    return inverse_rows(joined)


def shards(signal, grad_out, filter_taps, skip_gain):
    channels = filter_taps.shape[1]
    signal_rows = signal[0].astype(jnp.float32)
    grad_rows = grad_out[0].astype(jnp.float32)
    tap_half = filter_taps.shape[1] // 2
    columns = jnp.concatenate(
        [signal_rows, filter_taps[:, :tap_half], grad_rows, filter_taps[:, tap_half:]], axis=1
    )
    first, second = split_pairs(forward_spectra(columns))
    signal_spec = first[:, :, :, :channels]
    grad_spec = second[:, :, :, :channels]
    own_spec = jnp.concatenate([first[:, :, :, channels:], second[:, :, :, channels:]], axis=3)
    input_spec = jnp.stack(
        [
            grad_spec[0] * own_spec[0] + grad_spec[1] * own_spec[1],
            grad_spec[1] * own_spec[0] - grad_spec[0] * own_spec[1],
        ]
    )
    filter_terms = jnp.stack(
        [
            grad_spec[0] * signal_spec[0] + grad_spec[1] * signal_spec[1],
            grad_spec[1] * signal_spec[0] - grad_spec[0] * signal_spec[1],
        ]
    )
    summed = lax.psum(filter_terms, "batch")
    rows_back = invert_all(jnp.concatenate([input_spec, summed], axis=3))
    filter_grad = rows_back[:, channels:]
    input_grad = (rows_back[:, :channels] + skip_gain[None, :] * grad_rows).astype(jnp.bfloat16)
    return (input_grad[None], filter_grad)


def solution(mesh):
    return jax.shard_map(
        shards,
        mesh=mesh,
        in_specs=(P("batch", "seq", None), P("batch", "seq", None), P("seq", None), P()),
        out_specs=(P("batch", "seq", None), P("seq", None)),
        check_vma=False,
    )
```

profile of v0, /device:TPU:0, one launch (start us, length us, event | category | flops | bytes accessed | tf_op | source)
XLA Modules:
  0.0 231.8 jit_solution(8577959397815715858)
XLA Ops:
  7.2 1.0 fusion.173
  8.2 1.0 bitcast_convert_fusion
  9.2 0.1 maximum_bitcast_fusion
  9.2 1.7 copy.37
  10.9 7.3 %all-to-all-start = ((f32[1,256,768]{2,0,1:T(1,128)}), f32[1,256,768]{2,0,1:T(1,128)S(1)}, u32[]{:S(2)}, u32[]{:S(2)}) async-start(f32[1,256,768]{2,0,1:T(1,128)} %copy.37), calls=%async_computation | async-start | bytes 1572864 | tf_op jit(solution)/shard_map/all_to_all | solution.py:37
  18.3 0.2 fusion.58
  18.4 20.0 %all-to-all-done = f32[1,256,768]{2,0,1:T(1,128)S(1)} async-done(((f32[1,256,768]{2,0,1:T(1,128)}), f32[1,256,768]{2,0,1:T(1,128)S(1)}, u32[]{:S(2)}, u32[]{:S(2)}) %all-to-all-start) | async-done | bytes 786464 | tf_op jit(solution)/shard_map/all_to_all | solution.py:37
  38.5 0.1 fusion.171
  38.5 1.0 fusion.16
  39.5 1.0 fusion.20
  40.5 1.0 convolution_subtract_fusion.1
  41.4 1.1 add_bitcast_fusion
  42.6 0.1 pad_maximum_fusion.1
  42.7 1.7 copy.40
  44.4 3.6 %all-to-all-start.1 = ((f32[2,16,32,384]{3,2,0,1:T(8,128)}), f32[2,16,32,384]{3,2,0,1:T(8,128)S(1)}, u32[]{:S(2)}, u32[]{:S(2)}) async-start(f32[2,16,32,384]{3,2,0,1:T(8,128)} %copy.40), calls=%async_computation.1 | async-start | bytes 3145728 | tf_op jit(solution)/shard_map/all_to_all | solution.py:71
  48.0 0.2 all-reduce.2.cloned.1.call-start
  48.2 36.9 %all-to-all-done.1 = f32[2,16,32,384]{3,2,0,1:T(8,128)S(1)} async-done(((f32[2,16,32,384]{3,2,0,1:T(8,128)}), f32[2,16,32,384]{3,2,0,1:T(8,128)S(1)}, u32[]{:S(2)}, u32[]{:S(2)}) %all-to-all-start.1) | async-done | bytes 1572896 | tf_op jit(solution)/shard_map/all_to_all | solution.py:71
  85.1 0.1 copy.41
  85.3 0.1 fusion.169
  85.4 0.1 copy.42
  85.5 2.2 fusion.36
  87.7 0.1 copy.44
  87.7 2.2 fusion.34
  89.9 2.2 convolution_subtract_fusion
  92.1 2.2 convolution_add_fusion
  94.3 1.3 pad_maximum_fusion
  95.6 1.3 fusion.4
  96.9 11.2 %rev.4 = f32[2,2,256,384]{2,3,1,0:T(8,128)S(1)} reverse(f32[2,2,256,384]{2,3,1,0:T(8,128)} %pad_maximum_fusion), dimensions={1,2} | reverse | bytes 3145728 | tf_op jit(solution)/shard_map/rev | solution.py:85
  108.1 7.2 %slice.127 = f32[2,1,256,384]{2,3,1,0:T(8,128)} reverse(f32[2,1,256,384]{2,3,1,0:T(8,128)} %get-tuple-element.17), dimensions={2} | reverse | bytes 1572864 | tf_op jit(solution)/shard_map/slice | solution.py:84
  115.3 7.2 %slice.123 = f32[2,1,256,384]{2,3,0,1:T(8,128)} reverse(f32[2,1,256,384]{2,3,0,1:T(8,128)} %get-tuple-element.16), dimensions={2} | reverse | bytes 1572864 | tf_op jit(solution)/shard_map/slice | solution.py:83
  122.5 1.2 slice.150
  123.8 1.4 maximum_bitcast_fusion.1
  125.2 0.2 maximum_select_fusion
  125.4 0.4 fusion.13
  125.8 0.1 multiply_add_fusion
  125.9 0.7 copy-done
  126.7 0.2 copy-done.2
  126.9 1.0 pad_maximum_fusion.3
  128.0 0.1 fusion.167
  128.2 0.2 copy-done.1
  128.4 0.2 copy-done.3
  128.6 1.1 fusion.2
  129.7 33.8 %all-reduce.2.cloned.1.call-done = f32[2,2,256,256]{2,3,1,0:T(8,128)} async-done(((f32[2,2,256,256]{2,3,1,0:T(8,128)}), f32[2,2,256,256]{2,3,1,0:T(8,128)}) %all-reduce.2.cloned.1.call-update) | async-done | bytes 1048592 | tf_op jit(solution)/shard_map/psum | solution.py:167
  163.5 1.7 fusion.15
  165.2 1.6 fusion.30
  166.7 1.6 fusion.32
  168.3 1.6 convolution_add_fusion.2
  169.9 1.6 subtract_bitcast_fusion.1
  171.5 0.1 pad_maximum_fusion.4
  171.6 0.6 copy.49
  172.2 30.5 %all_to_all.51 = f32[2,2,256,256]{3,1,0,2:T(2,128)S(1)} all-to-all(f32[2,2,256,256]{3,1,0,2:T(2,128)S(1)} %copy.49), channel_id=1, replica_groups=mesh['batch'=4,'seq'=8] {'seq'}, dimensions={2} | all-to-all | bytes 2097152 | tf_op jit(solution)/shard_map/all_to_all | solution.py:119
  202.8 0.2 copy.50
  203.0 0.1 fusion.170
  203.1 0.4 copy.51
  203.5 0.4 squeeze.19
  203.9 0.4 fusion.69
  204.3 0.4 fusion.77
  204.7 0.4 copy.52
  205.1 0.4 squeeze.20
  205.5 0.4 fusion
  205.9 0.4 fusion.1
  206.4 0.3 copy.53
  206.7 17.4 %all_to_all.52 = f32[8,32,512]{2,1,0:T(8,128)S(1)} all-to-all(f32[8,32,512]{2,1,0:T(8,128)S(1)} %copy.53), channel_id=1, replica_groups=mesh['batch'=4,'seq'=8] {'seq'}, dimensions={0} | all-to-all | bytes 1048576 | tf_op jit(solution)/shard_map/all_to_all | solution.py:128
  224.2 0.8 fusion.172
  (21 shorter events, 0.2 us)
Async XLA Ops:
  10.9 27.5 %all-to-all-start = ((f32[1,256,768]{2,0,1:T(1,128)}), f32[1,256,768]{2,0,1:T(1,128)S(1)}, u32[]{:S(2)}, u32[]{:S(2)}) async-start(f32[1,256,768]{2,0,1:T(1,128)} %copy.37), calls=%async_computation | async-start | bytes 1572864 | tf_op jit(solution)/shard_map/all_to_all | solution.py:37
  44.4 40.8 %all-to-all-start.1 = ((f32[2,16,32,384]{3,2,0,1:T(8,128)}), f32[2,16,32,384]{3,2,0,1:T(8,128)S(1)}, u32[]{:S(2)}, u32[]{:S(2)}) async-start(f32[2,16,32,384]{3,2,0,1:T(8,128)} %copy.40), calls=%async_computation.1 | async-start | bytes 3145728 | tf_op jit(solution)/shard_map/all_to_all | solution.py:71
  48.0 115.5 %all-reduce.2.cloned.1.call-start = ((), (), s32[]{:S(2)}) async-start(), calls=%async_computation.4 | async-start | bytes 2097152 | tf_op jit(solution)/shard_map/psum | solution.py:167
  122.5 2.6 %copy-start.4 = (f32[2,1,256,384]{2,3,1,0:T(8,128)S(1)}, f32[2,1,256,384]{2,3,1,0:T(8,128)}, u32[]{:S(2)}) copy-start(f32[2,1,256,384]{2,3,1,0:T(8,128)} %slice.127) | copy-start | bytes 2359300
  125.8 0.9 copy-start
  125.8 1.1 copy-start.2
  126.9 1.5 copy-start.1
  126.9 1.7 copy-start.3
  206.3 17.8 %copy-start.5 = (bf16[1,256,256]{2,1,0:T(8,128)(2,1)S(1)}, bf16[1,256,256]{2,1,0:T(8,128)(2,1)}, u32[]{:S(2)}) copy-start(bf16[1,256,256]{2,1,0:T(8,128)(2,1)} %param.5) | copy-start | bytes 393220
  206.4 17.8 %copy-start.6 = (f32[256]{0:T(256)S(1)}, f32[256]{0:T(256)}, u32[]{:S(2)}) copy-start(f32[256]{0:T(256)} %param.7) | copy-start | bytes 3076
Sparse Core Ops, SparseCore 0:
  128.1 35.3 all-reduce.1
where the time goes:
time: 234 us; the launch traced here: 232 us
  waiting for transfers between devices  90.7 us (39%)
  blocking collectives  48 us (21%)
  local copies, waits for them, and re-layouts  36 us (15%)
  matrix products  20.8 us (9%)
  between operations  14.4 us (6%)
  starting transfers between devices  11.1 us (5%)
  other arithmetic  10.9 us (5%)
    all_to_all x1, waiting for transfers between devices, forward_spectra(): lax.all_to_all(rotated, 'seq', split_axis=1, concat_axis=2, tiled=True)  36.9 us
    psum x1, waiting for transfers between devices, shards(): summed = lax.psum(filter_terms, 'batch')  33.8 us
    all_to_all x1, blocking collectives, inverse_rows(): lax.all_to_all(rotated, 'seq', split_axis=2, concat_axis=1, tiled=True)  30.5 us
    dot_general x16, matrix products, contract(): return jnp.einsum(form, table, operand, precision=lax.Precision.HIGHEST)  20.8 us
    all_to_all x1, waiting for transfers between devices, forward_spectra(): lax.all_to_all(columns.reshape(1, row_count, columns.shape[1]), 'seq', sp...  20 us
    all_to_all x1, blocking collectives, inverse_rows(): lax.all_to_all(gathered, 'seq', split_axis=0, concat_axis=1, tiled=True)  17.4 us
    rev x1, local copies, waits for them, and re-layouts, split_pairs(): reversed_q[:, ::-1]  11.2 us
    slice x2, local copies, waits for them, and re-layouts, split_pairs(): zero_row = jnp.roll(reversed_q[:, 0], 1, axis=1)  8.44 us
  transfers between devices with their start and end apart: 3, of which 3 were waited for; matrix products, arithmetic and copies ran while one was open for 1% of the time, Pallas kernels for 0%

commit v1 on v0

--- a/solution.py
+++ b/solution.py
@@ -68,7 +68,10 @@
     inner_table = angle_table(row_count, row_count, row_count)
     cos_inner = jnp.cos(inner_table)
     sin_inner = jnp.sin(inner_table)
-    pieces = lax.all_to_all(rotated, "seq", split_axis=1, concat_axis=2, tiled=True)
+    pieces = jnp.concatenate(
+        lax.all_to_all(jnp.stack(jnp.split(rotated, lax.axis_size("seq"), axis=1)), "seq", 0, 0),
+        axis=2,
+    )
     real_sum = contract("qr,krw->kqw", cos_inner, pieces[0]) + contract(
         "qr,krw->kqw", sin_inner, pieces[1]
     )

time: 234 us -> 238 us (1.017)
  other arithmetic: 10.9 us -> 16.8 us
    unnamed x1 -> x8, other arithmetic: 1.25 us -> 6.51 us
where the time goes in v1:
time: 238 us; the launch traced here: 236 us
  waiting for transfers between devices  90.7 us (38%)
  blocking collectives  48 us (20%)
  local copies, waits for them, and re-layouts  35.6 us (15%)
  matrix products  19 us (8%)
  other arithmetic  16.8 us (7%)
  between operations  14.4 us (6%)
  starting transfers between devices  11.1 us (5%)
    all_to_all x1, waiting for transfers between devices, forward_spectra(): lax.all_to_all(jnp.stack(jnp.split(rotated, lax.axis_size('seq'), axis=1)...  36.9 us
    psum x1, waiting for transfers between devices, shards(): summed = lax.psum(filter_terms, 'batch')  33.8 us
    all_to_all x1, blocking collectives, inverse_rows(): lax.all_to_all(rotated, 'seq', split_axis=2, concat_axis=1, tiled=True)  30.5 us
    all_to_all x1, waiting for transfers between devices, forward_spectra(): lax.all_to_all(columns.reshape(1, row_count, columns.shape[1]), 'seq', sp...  20 us
    dot_general x16, matrix products, contract(): return jnp.einsum(form, table, operand, precision=lax.Precision.HIGHEST)  19 us
    all_to_all x1, blocking collectives, inverse_rows(): lax.all_to_all(gathered, 'seq', split_axis=0, concat_axis=1, tiled=True)  17.4 us
    rev x1, local copies, waits for them, and re-layouts, split_pairs(): reversed_q[:, ::-1]  11.2 us
    slice x2, local copies, waits for them, and re-layouts, split_pairs(): zero_row = jnp.roll(reversed_q[:, 0], 1, axis=1)  8.44 us
  transfers between devices with their start and end apart: 3, of which 3 were waited for; matrix products, arithmetic and copies ran while one was open for 1% of the time, Pallas kernels for 0%

profile of v1, /device:TPU:0, one launch (start us, length us, event | category | flops | bytes accessed | tf_op | source)
XLA Modules:
  0.0 235.6 jit_solution(18321370509550641613)
XLA Ops:
  7.2 1.0 fusion.196
  8.2 1.0 bitcast_convert_fusion
  9.2 1.7 copy.24
  10.9 7.3 %all-to-all-start = ((f32[1,256,768]{2,0,1:T(1,128)}), f32[1,256,768]{2,0,1:T(1,128)S(1)}, u32[]{:S(2)}, u32[]{:S(2)}) async-start(f32[1,256,768]{2,0,1:T(1,128)} %copy.24), calls=%async_computation | async-start | bytes 1572864 | tf_op jit(solution)/shard_map/all_to_all | solution.py:37
  18.3 0.2 fusion.81
  18.4 20.0 %all-to-all-done = f32[1,256,768]{2,0,1:T(1,128)S(1)} async-done(((f32[1,256,768]{2,0,1:T(1,128)}), f32[1,256,768]{2,0,1:T(1,128)S(1)}, u32[]{:S(2)}, u32[]{:S(2)}) %all-to-all-start) | async-done | bytes 786464 | tf_op jit(solution)/shard_map/all_to_all | solution.py:37
  38.5 1.0 fusion.16
  39.5 1.0 fusion.20
  40.5 1.0 convolution_subtract_fusion.1
  41.4 1.1 subtract_bitcast_fusion
  42.6 0.7 fusion.46
  43.3 0.8 fusion.49
  44.1 0.8 fusion.52
  44.8 0.8 fusion.55
  45.6 0.7 fusion.58
  46.3 0.7 fusion.61
  47.1 0.8 fusion.43
  47.8 0.8 fusion.63
  48.6 3.6 %all-to-all-start.1 = ((f32[8,2,2,32,384]{4,2,3,1,0:T(2,128)}), f32[8,2,2,32,384]{4,2,3,1,0:T(2,128)S(1)}, u32[]{:S(2)}, u32[]{:S(2)}) async-start(f32[8,2,2,32,384]{4,2,3,1,0:T(2,128)} %fusion.63), calls=%async_computation.1 | async-start | bytes 3145728 | tf_op jit(solution)/shard_map/all_to_all | solution.py:72
  52.2 0.2 all-reduce.2.cloned.1.call-start
  52.5 36.9 %all-to-all-done.1 = f32[8,2,2,32,384]{4,2,3,1,0:T(2,128)S(1)} async-done(((f32[8,2,2,32,384]{4,2,3,1,0:T(2,128)}), f32[8,2,2,32,384]{4,2,3,1,0:T(2,128)S(1)}, u32[]{:S(2)}, u32[]{:S(2)}) %all-to-all-start.1) | async-done | bytes 1572896 | tf_op jit(solution)/shard_map/all_to_all | solution.py:72
  89.4 0.7 fusion.192
  90.1 0.5 copy.27
  90.6 1.8 fusion.36
  92.3 0.5 copy.28
  92.8 1.8 fusion.34
  94.6 1.8 convolution_subtract_fusion
  96.4 1.8 convolution_add_fusion
  98.1 1.3 pad_maximum_fusion
  99.4 1.3 fusion.4
  100.7 11.2 %rev.4 = f32[2,2,256,384]{2,3,1,0:T(8,128)S(1)} reverse(f32[2,2,256,384]{2,3,1,0:T(8,128)} %pad_maximum_fusion), dimensions={1,2} | reverse | bytes 3145728 | tf_op jit(solution)/shard_map/rev | solution.py:88
  111.9 7.2 %slice.127 = f32[2,1,256,384]{2,3,1,0:T(8,128)} reverse(f32[2,1,256,384]{2,3,1,0:T(8,128)} %get-tuple-element.17), dimensions={2} | reverse | bytes 1572864 | tf_op jit(solution)/shard_map/slice | solution.py:87
  119.1 7.2 %slice.123 = f32[2,1,256,384]{2,3,0,1:T(8,128)} reverse(f32[2,1,256,384]{2,3,0,1:T(8,128)} %get-tuple-element.16), dimensions={2} | reverse | bytes 1572864 | tf_op jit(solution)/shard_map/slice | solution.py:86
  126.3 1.2 slice.150
  127.6 1.4 maximum_bitcast_fusion.1
  129.0 0.2 maximum_select_fusion
  129.2 0.4 fusion.13
  129.6 0.1 multiply_add_fusion
  129.7 0.7 copy-done
  130.4 0.2 copy-done.2
  130.7 1.0 pad_maximum_fusion.2
  132.0 0.2 copy-done.1
  132.2 0.2 copy-done.3
  132.4 1.1 fusion.2
  133.5 33.8 %all-reduce.2.cloned.1.call-done = f32[2,2,256,256]{2,3,1,0:T(8,128)} async-done(((f32[2,2,256,256]{2,3,1,0:T(8,128)}), f32[2,2,256,256]{2,3,1,0:T(8,128)}) %all-reduce.2.cloned.1.call-update) | async-done | bytes 1048592 | tf_op jit(solution)/shard_map/psum | solution.py:170
  167.3 1.7 fusion.15
  169.0 1.6 fusion.30
  170.5 1.6 fusion.32
  172.1 1.6 convolution_add_fusion.2
  173.7 1.6 subtract_bitcast_fusion.1
  175.4 0.6 copy.32
  176.0 30.5 %all_to_all.41 = f32[2,2,256,256]{3,1,0,2:T(2,128)S(1)} all-to-all(f32[2,2,256,256]{3,1,0,2:T(2,128)S(1)} %copy.32), channel_id=1, replica_groups=mesh['batch'=4,'seq'=8] {'seq'}, dimensions={2} | all-to-all | bytes 2097152 | tf_op jit(solution)/shard_map/all_to_all | solution.py:122
  206.6 0.2 copy.33
  206.9 0.4 copy.34
  207.3 0.4 squeeze.19
  207.7 0.4 fusion.92
  208.1 0.4 fusion.100
  208.5 0.4 copy.35
  208.9 0.4 squeeze.20
  209.3 0.4 fusion
  209.7 0.4 fusion.1
  210.2 0.3 copy.36
  210.5 17.4 %all_to_all.42 = f32[8,32,512]{2,1,0:T(8,128)S(1)} all-to-all(f32[8,32,512]{2,1,0:T(8,128)S(1)} %copy.36), channel_id=1, replica_groups=mesh['batch'=4,'seq'=8] {'seq'}, dimensions={0} | all-to-all | bytes 1048576 | tf_op jit(solution)/shard_map/all_to_all | solution.py:131
  228.0 0.8 fusion.195
  (26 shorter events, 0.6 us)
Async XLA Ops:
  10.9 27.5 %all-to-all-start = ((f32[1,256,768]{2,0,1:T(1,128)}), f32[1,256,768]{2,0,1:T(1,128)S(1)}, u32[]{:S(2)}, u32[]{:S(2)}) async-start(f32[1,256,768]{2,0,1:T(1,128)} %copy.24), calls=%async_computation | async-start | bytes 1572864 | tf_op jit(solution)/shard_map/all_to_all | solution.py:37
  48.6 40.8 %all-to-all-start.1 = ((f32[8,2,2,32,384]{4,2,3,1,0:T(2,128)}), f32[8,2,2,32,384]{4,2,3,1,0:T(2,128)S(1)}, u32[]{:S(2)}, u32[]{:S(2)}) async-start(f32[8,2,2,32,384]{4,2,3,1,0:T(2,128)} %fusion.63), calls=%async_computation.1 | async-start | bytes 3145728 | tf_op jit(solution)/shard_map/all_to_all | solution.py:72
  52.2 115.1 %all-reduce.2.cloned.1.call-start = ((), (), s32[]{:S(2)}) async-start(), calls=%async_computation.4 | async-start | bytes 2097152 | tf_op jit(solution)/shard_map/psum | solution.py:170
  126.3 2.6 %copy-start.4 = (f32[2,1,256,384]{2,3,1,0:T(8,128)S(1)}, f32[2,1,256,384]{2,3,1,0:T(8,128)}, u32[]{:S(2)}) copy-start(f32[2,1,256,384]{2,3,1,0:T(8,128)} %slice.127) | copy-start | bytes 2359300
  129.5 0.9 copy-start
  129.6 1.1 copy-start.2
  130.7 1.5 copy-start.1
  130.7 1.7 copy-start.3
  210.1 17.8 %copy-start.5 = (bf16[1,256,256]{2,1,0:T(8,128)(2,1)S(1)}, bf16[1,256,256]{2,1,0:T(8,128)(2,1)}, u32[]{:S(2)}) copy-start(bf16[1,256,256]{2,1,0:T(8,128)(2,1)} %param.5) | copy-start | bytes 393220
  210.2 17.8 %copy-start.6 = (f32[256]{0:T(256)S(1)}, f32[256]{0:T(256)}, u32[]{:S(2)}) copy-start(f32[256]{0:T(256)} %param.7) | copy-start | bytes 3076
Sparse Core Ops, SparseCore 0:
  131.9 35.3 all-reduce.1
